TPU v7x, 32 devices: a whole 2x2x4 slice. The times are simulated.
32 devices in a mesh: dp: 4 (over y, x), seq: 8 (over z, core).
Axes of the slice: x: 2, y: 2, z: 4, core: 2. Of those that a mesh axis runs over, the one named last changes fastest.
Arguments:
- queries: bfloat16 [4, 1024, 2048], P('dp', 'seq'), may hold values from -6 to 6
- key_vectors: bfloat16 [4, 1024, 2048], P('dp', 'seq'), may hold values from -6 to 6
- values: bfloat16 [4, 1024, 2048], P('dp', 'seq'), may hold values from -6 to 6
- out_grad: bfloat16 [4, 1024, 2048], P('dp', 'seq'), may hold values from -6 to 6
- inputs: bfloat16 [4, 1024, 2048], P('dp', 'seq'), may hold values from -6 to 6
Outputs:
- query_grad: bfloat16 [4, 1024, 2048], P('dp', 'seq')
- key_grad: bfloat16 [4, 1024, 2048], P('dp', 'seq')
- value_grad: bfloat16 [4, 1024, 2048], P('dp', 'seq')
- weight_grad: float32 [2048, 2048], P('dp', 'seq')
All inputs are finite; a program needn't handle non-finite values.
Results may differ from a plain program's by a relative error of at most 0.025.
Values may be sent and summed in bfloat16 or wider, within the bound.
No kernel may reach another device: no remote copies, remote signals or barrier semaphores. Data moves between devices by JAX's collectives and lax.ppermute only.
A program may use at most 128 MiB of HBM per device.

v0:
```python
import jax
import jax.numpy as jnp
from jax import lax
from jax.sharding import PartitionSpec as P

HD = 128


def partner(value, axis, apart):
    return lax.ppermute(value, axis, [(i, i ^ 1 << apart) for i in range(lax.axis_size(axis))])


def body(queries, key_vectors, values, out_grad, inputs):
    seq_count = lax.axis_size("seq")
    groups = seq_count // 2
    parity = lax.axis_index("seq") % 2
    is_even = parity == 0
    tok_rows = queries.shape[1]
    half_rows = tok_rows // 2
    width = queries.shape[2]
    group_width = 2 * width // seq_count
    heads_here = group_width // HD
    model_width = inputs.shape[2]
    own_rows = seq_count * half_rows
    length = 2 * own_rows
    doc_rows = own_rows // 4
    block_rows = min(doc_rows, max(256, length // 16))
    block_count = own_rows // block_rows
    scale = HD ** (-0.5)

    def to_heads(array):
        return (
            array[0]
            .reshape(half_rows, 2, groups, group_width)
            .transpose(0, 2, 1, 3)
            .reshape(half_rows, seq_count, group_width)
        )

    moved = (
        lax.all_to_all(to_heads(queries), "seq", split_axis=1, concat_axis=0, tiled=True),
        lax.all_to_all(to_heads(key_vectors), "seq", split_axis=1, concat_axis=0, tiled=True),
        lax.all_to_all(to_heads(values), "seq", split_axis=1, concat_axis=0, tiled=True),
        lax.all_to_all(to_heads(out_grad), "seq", split_axis=1, concat_axis=0, tiled=True),
    )
    q_rows = moved[0].reshape(own_rows, group_width)
    k_rows = moved[1].reshape(own_rows, group_width)
    v_rows = moved[2].reshape(own_rows, group_width)
    g_rows = moved[3].reshape(own_rows, group_width)
    k_other, v_other = partner((k_rows, v_rows), "seq", 0)

    def in_order(mine, theirs):
        even_rows = jnp.where(is_even, mine, theirs)
        odd_rows = jnp.where(is_even, theirs, mine)
        return jnp.stack([even_rows, odd_rows], axis=1).reshape(2 * mine.shape[0], mine.shape[1])

    key_all = in_order(k_rows, k_other).reshape(length, heads_here, HD)
    value_all = in_order(v_rows, v_other).reshape(length, heads_here, HD)
    query_heads = q_rows.reshape(own_rows, heads_here, HD)
    grad_heads = g_rows.reshape(own_rows, heads_here, HD)
    key_total = jnp.zeros((length, heads_here, HD), jnp.float32)
    value_total = jnp.zeros((length, heads_here, HD), jnp.float32)
    query_parts = []
    for block in range(block_count):
        start = block * block_rows
        stop = start + block_rows
        low = 2 * (start // doc_rows * doc_rows)
        high = 2 * stop
        query_block = query_heads[start:stop]
        grad_block = grad_heads[start:stop]
        key_block = key_all[low:high]
        value_block = value_all[low:high]
        scores = (
            jnp.einsum("qhd,khd->hqk", query_block, key_block, preferred_element_type=jnp.float32)
            * scale
        )
        query_pos = 2 * (start + jnp.arange(block_rows, dtype=jnp.int32)) + parity
        key_pos = low + jnp.arange(high - low, dtype=jnp.int32)
        visible = key_pos[None, :] <= query_pos[:, None]
        scores = jnp.where(visible[None], scores, -jnp.inf)
        top = jnp.max(scores, axis=2, keepdims=True)
        weights = jnp.exp(scores - top)
        probs = weights / jnp.sum(weights, axis=2, keepdims=True)
        probs_low = probs.astype(jnp.bfloat16)
        dprob = jnp.einsum(
            "qhd,khd->hqk", grad_block, value_block, preferred_element_type=jnp.float32
        )
        delta = jnp.sum(probs * dprob, axis=2, keepdims=True)
        dscore = (probs * (dprob - delta) * scale).astype(jnp.bfloat16)
        query_parts.append(
            jnp.einsum(
                "hqk,khd->qhd", dscore, key_block, preferred_element_type=jnp.float32
            ).astype(jnp.bfloat16)
        )
        key_total = key_total.at[low:high].add(
            jnp.einsum("hqk,qhd->khd", dscore, query_block, preferred_element_type=jnp.float32)
        )
        value_total = value_total.at[low:high].add(
            jnp.einsum("hqk,qhd->khd", probs_low, grad_block, preferred_element_type=jnp.float32)
        )
    query_grad = jnp.concatenate(query_parts, axis=0).reshape(own_rows, group_width)

    def by_parity(total):
        paired = total.reshape(own_rows, 2, group_width)
        mine = jnp.where(is_even, paired[:, 0], paired[:, 1])
        theirs = jnp.where(is_even, paired[:, 1], paired[:, 0])
        return (mine.astype(jnp.bfloat16), theirs.astype(jnp.bfloat16))

    key_mine, key_theirs = by_parity(key_total)
    value_mine, value_theirs = by_parity(value_total)
    key_back, value_back = partner((key_theirs, value_theirs), "seq", 0)
    key_grad = (key_mine.astype(jnp.float32) + key_back.astype(jnp.float32)).astype(jnp.bfloat16)
    value_grad = (value_mine.astype(jnp.float32) + value_back.astype(jnp.float32)).astype(
        jnp.bfloat16
    )
    spread = jnp.broadcast_to(
        inputs[0].reshape(half_rows, 1, 2, model_width), (half_rows, groups, 2, model_width)
    ).reshape(half_rows, seq_count, model_width)
    input_rows = lax.all_to_all(spread, "seq", split_axis=1, concat_axis=0, tiled=True).reshape(
        own_rows, model_width
    )
    term = jnp.einsum("td,tc->dc", input_rows, value_grad, preferred_element_type=jnp.float32)
    halves = term.reshape(term.shape[0], 2, term.shape[1] // 2)
    mine = jnp.where(is_even, halves[:, 0], halves[:, 1])
    theirs = jnp.where(is_even, halves[:, 1], halves[:, 0])
    mine, theirs = (mine, theirs)
    received = partner(theirs.astype(jnp.bfloat16), "seq", 0).astype(theirs.dtype)
    weight_grad = lax.psum_scatter(
        (mine + received).astype(jnp.bfloat16), "dp", scatter_dimension=0, tiled=True
    ).astype(jnp.float32)

    def to_tokens(array):
        return array.reshape(seq_count, half_rows, 1, group_width)

    def from_heads(array):
        return (
            array.reshape(half_rows, groups, 2, group_width)
            .transpose(0, 2, 1, 3)
            .reshape(1, tok_rows, width)
        )

    returned = (
        lax.all_to_all(to_tokens(query_grad), "seq", split_axis=0, concat_axis=2, tiled=True),
        lax.all_to_all(to_tokens(key_grad), "seq", split_axis=0, concat_axis=2, tiled=True),
        lax.all_to_all(to_tokens(value_grad), "seq", split_axis=0, concat_axis=2, tiled=True),
    )
    return (from_heads(returned[0]), from_heads(returned[1]), from_heads(returned[2]), weight_grad)


def solution(mesh):
    return jax.shard_map(
        body,
        mesh=mesh,
        in_specs=(
            P("dp", "seq", None),
            P("dp", "seq", None),
            P("dp", "seq", None),
            P("dp", "seq", None),
            P("dp", "seq", None),
        ),
        out_specs=(
            P("dp", "seq", None),
            P("dp", "seq", None),
            P("dp", "seq", None),
            P("dp", "seq"),
        ),
        check_vma=False,
    )
```

profile of v0, /device:TPU:0, one launch (start us, length us, event | category | flops | bytes accessed | tf_op | source)
XLA Modules:
  0.0 255.6 jit_solution(17739342030090548654)
XLA Ops:
  9.6 6.5 %all-to-all-start.2 = ((bf16[64,8,512]{2,0,1:T(8,128)(2,1)}), bf16[64,8,512]{2,0,1:T(8,128)(2,1)S(1)}, u32[]{:S(2)}, u32[]{:S(2)}) async-start(bf16[64,8,512]{2,0,1:T(8,128)(2,1)} %bitcast.15), calls=%async_computation.2 | async-start | bytes 1048576 | tf_op jit(solution)/shard_map/all_to_all | solution.py:42
  17.4 14.0 %all-to-all-done.2 = bf16[64,8,512]{2,0,1:T(8,128)(2,1)S(1)} async-done(((bf16[64,8,512]{2,0,1:T(8,128)(2,1)}), bf16[64,8,512]{2,0,1:T(8,128)(2,1)S(1)}, u32[]{:S(2)}, u32[]{:S(2)}) %all-to-all-start.2) | async-done | bytes 524320 | tf_op jit(solution)/shard_map/all_to_all | solution.py:42
  31.4 3.6 %all-to-all-start.3 = ((bf16[64,8,512]{2,0,1:T(8,128)(2,1)}), bf16[64,8,512]{2,0,1:T(8,128)(2,1)S(1)}, u32[]{:S(2)}, u32[]{:S(2)}) async-start(bf16[64,8,512]{2,0,1:T(8,128)(2,1)} %bitcast.24), calls=%async_computation.3 | async-start | bytes 1048576 | tf_op jit(solution)/shard_map/all_to_all | solution.py:43
  36.4 13.9 %all-to-all-done.3 = bf16[64,8,512]{2,0,1:T(8,128)(2,1)S(1)} async-done(((bf16[64,8,512]{2,0,1:T(8,128)(2,1)}), bf16[64,8,512]{2,0,1:T(8,128)(2,1)S(1)}, u32[]{:S(2)}, u32[]{:S(2)}) %all-to-all-start.3) | async-done | bytes 524320 | tf_op jit(solution)/shard_map/all_to_all | solution.py:43
  50.4 3.5 %all-to-all-start = ((bf16[64,8,512]{2,0,1:T(8,128)(2,1)}), bf16[64,8,512]{2,0,1:T(8,128)(2,1)S(1)}, u32[]{:S(2)}, u32[]{:S(2)}) async-start(bf16[64,8,512]{2,0,1:T(8,128)(2,1)} %bitcast.1), calls=%async_computation | async-start | bytes 1048576 | tf_op jit(solution)/shard_map/all_to_all | solution.py:41
  55.9 13.2 %all-to-all-done = bf16[64,8,512]{2,0,1:T(8,128)(2,1)S(1)} async-done(((bf16[64,8,512]{2,0,1:T(8,128)(2,1)}), bf16[64,8,512]{2,0,1:T(8,128)(2,1)S(1)}, u32[]{:S(2)}, u32[]{:S(2)}) %all-to-all-start) | async-done | bytes 524320 | tf_op jit(solution)/shard_map/all_to_all | solution.py:41
  69.1 3.5 %all-to-all-start.1 = ((bf16[64,8,512]{2,0,1:T(8,128)(2,1)}), bf16[64,8,512]{2,0,1:T(8,128)(2,1)S(1)}, u32[]{:S(2)}, u32[]{:S(2)}) async-start(bf16[64,8,512]{2,0,1:T(8,128)(2,1)} %bitcast.10), calls=%async_computation.1 | async-start | bytes 1048576 | tf_op jit(solution)/shard_map/all_to_all | solution.py:40
  77.6 10.3 %all-to-all-done.1 = bf16[64,8,512]{2,0,1:T(8,128)(2,1)S(1)} async-done(((bf16[64,8,512]{2,0,1:T(8,128)(2,1)}), bf16[64,8,512]{2,0,1:T(8,128)(2,1)S(1)}, u32[]{:S(2)}, u32[]{:S(2)}) %all-to-all-start.1) | async-done | bytes 524320 | tf_op jit(solution)/shard_map/all_to_all | solution.py:40
  87.9 1.6 broadcast_in_dim.67
  89.5 3.8 %all-to-all-start.7 = ((bf16[64,8,2048]{2,0,1:T(8,128)(2,1)}), bf16[64,8,2048]{2,0,1:T(8,128)(2,1)S(1)}, u32[]{:S(2)}, u32[]{:S(2)}) async-start(bf16[64,8,2048]{2,0,1:T(8,128)(2,1)} %bitcast.65), calls=%async_computation.7 | async-start | bytes 4194304 | tf_op jit(solution)/shard_map/all_to_all | solution.py:118
  93.3 1.9 fusion.219
  96.8 1.6 slice.325
  100.7 1.6 slice.313
  110.2 2.1 fusion.236
  112.3 2.3 convolution_bitcast_fusion.3
  114.6 2.5 scatter-add.34
  117.1 2.1 fusion.221
  119.2 2.2 fusion.231
  121.4 2.4 fusion.17
  124.2 1.9 fusion.226
  126.1 2.4 fusion.24
  133.6 2.5 fusion.26
  136.2 3.9 %copy.167 = bf16[1024,4,128]{2,1,0:T(4,128)(2,1)} copy(f32[1024,4,128]{2,0,1:T(8,128)} %fusion.26) | data formatting | bytes 3145728 | tf_op jit(solution)/shard_map/scatter-add | solution.py:97
  141.6 3.0 %fusion.60 = (bf16[512,1,512]{2,1,0:T(2,128)(2,1)S(1)}, f32[512,1,512]{2,1,0:T(1,128)}) fusion(pred[]{:T(512)S(6)} %eq.5, bf16[512,2,512]{2,1,0:T(2,128)(2,1)S(1)} %reshape.498), kind=kLoop, calls=%fused_computation.98 | loop fusion | flops 786432 | bytes 2621441 | tf_op jit(solution)/shard_map/convert_element_type | solution.py:106
  146.0 2.4 fusion.54
  148.5 2.0 convolution_bitcast_fusion.9
  150.4 2.7 %fusion.53 = bf16[128,4,128]{2,0,1:T(8,128)(2,1)} fusion(f32[4,128,256]{1,2,0:T(8,128)} %convolution_bitcast_fusion.9, bf16[256,4,128]{2,1,0:T(4,128)(2,1)} %copy-done.18, f32[4,128,256]{1,2,0:T(8,128)} %get-tuple-element.129, f32[4,128]{1,0:T(4,128)S(1)} %get-tuple-element.128), kind=kOutput, calls=%fused_computation.91 | convolution fusion | flops 34538240 | bytes 1443840 | tf_op jit(solution)/shard_map/hqk,khd->qhd/dot_general | solution.py:90
  154.2 2.7 %fusion.52 = bf16[128,4,128]{2,0,1:T(8,128)(2,1)} fusion(f32[4,128,256]{1,2,0:T(8,128)} %convolution_bitcast_fusion.10, bf16[256,4,128]{2,1,0:T(4,128)(2,1)} %slice.311, f32[4,128,256]{1,2,0:T(8,128)} %get-tuple-element.131, f32[4,128]{1,0:T(4,128)S(1)} %get-tuple-element.130), kind=kOutput, calls=%fused_computation.90 | convolution fusion | flops 34538240 | bytes 1443840 | tf_op jit(solution)/shard_map/hqk,khd->qhd/dot_general | solution.py:90
  157.2 1.6 fusion.51
  160.3 2.4 convolution_bitcast_fusion.7
  162.7 2.6 %scatter-add.26 = f32[1024,4,128]{2,0,1:T(8,128)} pad(f32[256,4,128]{2,0,1:T(8,128)} %convolution_bitcast_fusion.7, f32[]{:T(128)} %constant.216.clone.1), padding=0_768x0_0x0_0 | pad | bytes 2621444 | tf_op jit(solution)/shard_map/scatter-add | solution.py:94
  165.3 2.8 %fusion.18 = f32[1024,4,128]{2,0,1:T(8,128)} fusion(f32[1024,4,128]{2,0,1:T(8,128)} %scatter-add.26, f32[4,128,256]{1,2,0:T(8,128)} %convolution_bitcast_fusion.10, bf16[128,4,128]{2,1,0:T(4,128)(2,1)S(1)} %copy-done.23, f32[4,128,256]{1,2,0:T(8,128)} %get-tuple-element.131, f32[4,128]{1,0:T(4,128)S(1)} %get-tuple-element.130), kind=kOutput, calls=%fused_computation.43 | convolution fusion | flops 34472704 | bytes 2756608 | tf_op jit(solution)/shard_map/hqk,qhd->khd/dot_general | solution.py:95
  168.1 2.1 fusion.62
  170.1 4.8 %all-to-all-start.4 = ((bf16[8,64,1,512]{3,1,2,0:T(8,128)(2,1)}), bf16[8,64,1,512]{3,1,2,0:T(8,128)(2,1)}, u32[]{:S(2)}, u32[]{:S(2)}) async-start(bf16[8,64,1,512]{3,1,2,0:T(8,128)(2,1)} %bitcast.239), calls=%async_computation.4 | async-start | bytes 1048576 | tf_op jit(solution)/shard_map/all_to_all | solution.py:142
  174.9 2.3 fusion.241
  177.3 2.2 fusion.218
  179.5 1.9 copy.182
  181.4 2.9 %copy.181 = f32[2048,1,256]{2,0,1:T(8,128)} copy(f32[2048,1,256]{0,2,1:T(8,128)} %get-tuple-element.100) | data formatting | bytes 4194304
  185.6 2.1 collective-permute-start.4
  187.7 2.8 %fusion.20 = f32[1024,4,128]{2,0,1:T(8,128)} fusion(f32[1024,4,128]{2,0,1:T(8,128)} %fusion.18, f32[4,128,256]{1,2,0:T(8,128)} %convolution_bitcast_fusion.9, bf16[128,4,128]{2,1,0:T(4,128)(2,1)S(1)} %copy-done.22, f32[4,128,256]{1,2,0:T(8,128)} %get-tuple-element.129, f32[4,128]{1,0:T(4,128)S(1)} %get-tuple-element.128), kind=kOutput, calls=%fused_computation.50 | convolution fusion | flops 34603776 | bytes 3280896 | tf_op jit(solution)/shard_map/hqk,qhd->khd/dot_general | solution.py:95
  190.5 2.8 %fusion.22 = f32[1024,4,128]{2,0,1:T(8,128)} fusion(f32[1024,4,128]{2,0,1:T(8,128)} %fusion.20, f32[4,128,256]{1,2,0:T(8,128)} %copy-done.7, bf16[128,4,128]{2,1,0:T(4,128)(2,1)S(1)} %copy-done.20, f32[4,128,256]{1,2,0:T(8,128)} %get-tuple-element.127, f32[4,128]{1,0:T(4,128)S(1)} %get-tuple-element.126), kind=kOutput, calls=%fused_computation.52 | convolution fusion | flops 34603776 | bytes 3280896 | tf_op jit(solution)/shard_map/hqk,qhd->khd/dot_general | solution.py:95
  193.3 3.9 %copy.160 = bf16[1024,4,128]{2,1,0:T(4,128)(2,1)} copy(f32[1024,4,128]{2,0,1:T(8,128)} %fusion.22) | data formatting | bytes 3145728 | tf_op jit(solution)/shard_map/scatter-add | solution.py:94
  198.7 3.0 %fusion.57 = (bf16[512,1,512]{2,1,0:T(2,128)(2,1)S(1)}, f32[512,1,512]{2,1,0:T(1,128)}) fusion(pred[]{:T(512)S(6)} %eq.5, bf16[512,2,512]{2,1,0:T(2,128)(2,1)S(1)} %reshape.494), kind=kLoop, calls=%fused_computation.95 | loop fusion | flops 786432 | bytes 2621441 | tf_op jit(solution)/shard_map/convert_element_type | solution.py:106
  202.7 2.7 %fusion.8 = bf16[2048,256]{1,0:T(8,128)(2,1)} fusion(bf16[2048,256]{1,0:T(8,128)(2,1)} %collective-permute-done.4, f32[2048,1,256]{2,0,1:T(8,128)S(1)} %copy-done, f32[2048,1,256]{2,0,1:T(8,128)S(1)} %copy.182, pred[]{:T(512)S(6)} %eq.5), kind=kLoop, calls=%fused_computation.9 | loop fusion | flops 2097152 | bytes 6291457 | tf_op jit(solution)/shard_map/convert_element_type | solution.py:128
  206.7 19.9 %all_to_all.120 = bf16[8,64,1,512]{3,1,2,0:T(8,128)(2,1)S(1)} all-to-all(bf16[8,64,1,512]{3,1,2,0:T(8,128)(2,1)S(1)} %bitcast.248), channel_id=1, replica_groups=mesh['dp'=4,'seq'=8] {'seq'}, dimensions={0} | all-to-all | bytes 1048576 | tf_op jit(solution)/shard_map/all_to_all | solution.py:143
  226.6 3.8 %all-to-all-start.6 = ((bf16[8,64,1,512]{3,1,2,0:T(8,128)(2,1)}), bf16[8,64,1,512]{3,1,2,0:T(8,128)(2,1)S(1)}, u32[]{:S(2)}, u32[]{:S(2)}) async-start(bf16[8,64,1,512]{3,1,2,0:T(8,128)(2,1)} %bitcast.60), calls=%async_computation.6 | async-start | bytes 1048576 | tf_op jit(solution)/shard_map/all_to_all | solution.py:144
  234.6 10.8 %all-to-all-done.6 = bf16[8,64,1,512]{3,1,2,0:T(8,128)(2,1)S(1)} async-done(((bf16[8,64,1,512]{3,1,2,0:T(8,128)(2,1)}), bf16[8,64,1,512]{3,1,2,0:T(8,128)(2,1)S(1)}, u32[]{:S(2)}, u32[]{:S(2)}) %all-to-all-start.6) | async-done | bytes 524320 | tf_op jit(solution)/shard_map/all_to_all | solution.py:144
  247.0 1.8 convert_element_type.141
  (134 shorter events, 45.7 us)
Async XLA Ops:
  7.2 8.9 %copy-start.12 = (bf16[1,128,2048]{2,1,0:T(8,128)(2,1)S(1)}, bf16[1,128,2048]{2,1,0:T(8,128)(2,1)}, u32[]{:S(2)}) copy-start(bf16[1,128,2048]{2,1,0:T(8,128)(2,1)} %param.24) | copy-start | bytes 1572868
  9.6 25.5 %copy-start.13 = (bf16[1,128,2048]{2,1,0:T(8,128)(2,1)S(1)}, bf16[1,128,2048]{2,1,0:T(8,128)(2,1)}, u32[]{:S(2)}) copy-start(bf16[1,128,2048]{2,1,0:T(8,128)(2,1)} %param.22) | copy-start | bytes 1572868
  9.6 21.8 %all-to-all-start.2 = ((bf16[64,8,512]{2,0,1:T(8,128)(2,1)}), bf16[64,8,512]{2,0,1:T(8,128)(2,1)S(1)}, u32[]{:S(2)}, u32[]{:S(2)}) async-start(bf16[64,8,512]{2,0,1:T(8,128)(2,1)} %bitcast.15), calls=%async_computation.2 | async-start | bytes 1048576 | tf_op jit(solution)/shard_map/all_to_all | solution.py:42
  31.4 22.4 %copy-start.14 = (bf16[1,128,2048]{2,1,0:T(8,128)(2,1)S(1)}, bf16[1,128,2048]{2,1,0:T(8,128)(2,1)}, u32[]{:S(2)}) copy-start(bf16[1,128,2048]{2,1,0:T(8,128)(2,1)} %param.21) | copy-start | bytes 1572868
  31.4 18.9 %all-to-all-start.3 = ((bf16[64,8,512]{2,0,1:T(8,128)(2,1)}), bf16[64,8,512]{2,0,1:T(8,128)(2,1)S(1)}, u32[]{:S(2)}, u32[]{:S(2)}) async-start(bf16[64,8,512]{2,0,1:T(8,128)(2,1)} %bitcast.24), calls=%async_computation.3 | async-start | bytes 1048576 | tf_op jit(solution)/shard_map/all_to_all | solution.py:43
  50.4 18.8 %all-to-all-start = ((bf16[64,8,512]{2,0,1:T(8,128)(2,1)}), bf16[64,8,512]{2,0,1:T(8,128)(2,1)S(1)}, u32[]{:S(2)}, u32[]{:S(2)}) async-start(bf16[64,8,512]{2,0,1:T(8,128)(2,1)} %bitcast.1), calls=%async_computation | async-start | bytes 1048576 | tf_op jit(solution)/shard_map/all_to_all | solution.py:41
  69.1 18.8 %all-to-all-start.1 = ((bf16[64,8,512]{2,0,1:T(8,128)(2,1)}), bf16[64,8,512]{2,0,1:T(8,128)(2,1)S(1)}, u32[]{:S(2)}, u32[]{:S(2)}) async-start(bf16[64,8,512]{2,0,1:T(8,128)(2,1)} %bitcast.10), calls=%async_computation.1 | async-start | bytes 1048576 | tf_op jit(solution)/shard_map/all_to_all | solution.py:40
  74.1 30.5 %collective-permute-start = (bf16[512,512]{1,0:T(8,128)(2,1)S(1)}, bf16[512,512]{1,0:T(8,128)(2,1)}, u32[]{:S(2)}, u32[]{:S(2)}) collective-permute-start(bf16[512,512]{1,0:T(8,128)(2,1)S(1)} %bitcast.238), channel_id=1, source_target_pairs={{0,1},{1,0},{2,3},{3,2},{4,5},{5,4},{6,7},{7,6},{8,9},{9,8},{10,11... | collective-permute-start | bytes 1572872 | tf_op jit(solution)/shard_map/ppermute | solution.py:10
  76.6 51.8 %collective-permute-start.1 = (bf16[512,512]{1,0:T(8,128)(2,1)S(1)}, bf16[512,512]{1,0:T(8,128)(2,1)}, u32[]{:S(2)}, u32[]{:S(2)}) collective-permute-start(bf16[512,512]{1,0:T(8,128)(2,1)S(1)} %bitcast.237), channel_id=1, source_target_pairs={{0,1},{1,0},{2,3},{3,2},{4,5},{5,4},{6,7},{7,6},{8,9},{9,8},{10,11... | collective-permute-start | bytes 1572872 | tf_op jit(solution)/shard_map/ppermute | solution.py:10
  87.9 1.6 copy-start.3
  89.5 80.6 %all-to-all-start.7 = ((bf16[64,8,2048]{2,0,1:T(8,128)(2,1)}), bf16[64,8,2048]{2,0,1:T(8,128)(2,1)S(1)}, u32[]{:S(2)}, u32[]{:S(2)}) async-start(bf16[64,8,2048]{2,0,1:T(8,128)(2,1)} %bitcast.65), calls=%async_computation.7 | async-start | bytes 4194304 | tf_op jit(solution)/shard_map/all_to_all | solution.py:118
  110.1 6.9 %copy-start.15 = (bf16[256,4,128]{2,1,0:T(4,128)(2,1)}, bf16[256,4,128]{2,1,0:T(4,128)(2,1)S(1)}, u32[]{:S(2)}) copy-start(bf16[256,4,128]{2,1,0:T(4,128)(2,1)S(1)} %slice.303) | copy-start | bytes 786436
  112.3 4.8 %copy-start.19 = (bf16[128,4,128]{2,1,0:T(4,128)(2,1)S(1)}, bf16[128,4,128]{2,1,0:T(4,128)(2,1)}, u32[]{:S(2)}) copy-start(bf16[128,4,128]{2,1,0:T(4,128)(2,1)} %slice.329) | copy-start | bytes 393220
  117.1 4.3 %copy-start.9 = (bf16[128,4,128]{2,1,0:T(4,128)(2,1)S(1)}, bf16[128,4,128]{2,1,0:T(4,128)(2,1)}, u32[]{:S(2)}) copy-start(bf16[128,4,128]{2,1,0:T(4,128)(2,1)} %slice.317) | copy-start | bytes 393220
  121.4 2.8 %copy-start.21 = (bf16[128,4,128]{2,1,0:T(4,128)(2,1)S(1)}, bf16[128,4,128]{2,1,0:T(4,128)(2,1)}, u32[]{:S(2)}) copy-start(bf16[128,4,128]{2,1,0:T(4,128)(2,1)} %slice.321) | copy-start | bytes 393220
  121.4 4.7 %copy-start.11 = (bf16[128,4,128]{2,1,0:T(4,128)(2,1)S(1)}, bf16[128,4,128]{2,1,0:T(4,128)(2,1)}, u32[]{:S(2)}) copy-start(bf16[128,4,128]{2,1,0:T(4,128)(2,1)} %slice.325) | copy-start | bytes 393220
  124.2 4.3 %copy-start.18 = (bf16[256,4,128]{2,1,0:T(4,128)(2,1)}, bf16[256,4,128]{2,1,0:T(4,128)(2,1)S(1)}, u32[]{:S(2)}) copy-start(bf16[256,4,128]{2,1,0:T(4,128)(2,1)S(1)} %slice.319) | copy-start | bytes 786436
  141.5 4.2 %copy-start.6 = (bf16[256,4,128]{2,1,0:T(4,128)(2,1)S(1)}, bf16[256,4,128]{2,1,0:T(4,128)(2,1)}, u32[]{:S(2)}) copy-start(bf16[256,4,128]{2,1,0:T(4,128)(2,1)} %slice.331) | copy-start | bytes 786436
  144.6 1.4 copy-start.17
  145.5 2.9 %copy-start.5 = (bf16[256,4,128]{2,1,0:T(4,128)(2,1)S(1)}, bf16[256,4,128]{2,1,0:T(4,128)(2,1)}, u32[]{:S(2)}) copy-start(bf16[256,4,128]{2,1,0:T(4,128)(2,1)} %slice.323) | copy-start | bytes 786436
  145.5 22.5 %collective-permute-start.3 = (bf16[512,512]{1,0:T(8,128)(2,1)}, bf16[512,512]{1,0:T(8,128)(2,1)}, u32[]{:S(2)}, u32[]{:S(2)}) collective-permute-start(bf16[512,512]{1,0:T(8,128)(2,1)} %bitcast.233), channel_id=1, source_target_pairs={{0,1},{1,0},{2,3},{3,2},{4,5},{5,4},{6,7},{7,6},{8,9},{9,8},{10,11... | collective-permute-start | bytes 1572872 | tf_op jit(solution)/shard_map/ppermute | solution.py:10
  146.0 7.2 %copy-start.7 = (f32[4,128,256]{1,2,0:T(8,128)}, f32[4,128,256]{1,2,0:T(8,128)S(1)}, u32[]{:S(2)}) copy-start(f32[4,128,256]{1,2,0:T(8,128)S(1)} %convolution_bitcast_fusion.8) | copy-start | bytes 1572868
  148.5 4.7 %copy-start.4 = (bf16[256,4,128]{2,1,0:T(4,128)(2,1)S(1)}, bf16[256,4,128]{2,1,0:T(4,128)(2,1)}, u32[]{:S(2)}) copy-start(bf16[256,4,128]{2,1,0:T(4,128)(2,1)} %slice.315) | copy-start | bytes 786436
  148.5 4.7 %copy-start.10 = (bf16[128,4,128]{2,1,0:T(4,128)(2,1)S(1)}, bf16[128,4,128]{2,1,0:T(4,128)(2,1)}, u32[]{:S(2)}) copy-start(bf16[128,4,128]{2,1,0:T(4,128)(2,1)} %slice.317) | copy-start | bytes 393220
  153.2 3.8 %copy-start.8 = (bf16[128,4,128]{2,1,0:T(4,128)(2,1)S(1)}, bf16[128,4,128]{2,1,0:T(4,128)(2,1)}, u32[]{:S(2)}) copy-start(bf16[128,4,128]{2,1,0:T(4,128)(2,1)} %slice.309) | copy-start | bytes 393220
  154.2 3.0 %copy-start.16 = (bf16[256,4,128]{2,1,0:T(4,128)(2,1)S(1)}, bf16[256,4,128]{2,1,0:T(4,128)(2,1)}, u32[]{:S(2)}) copy-start(bf16[256,4,128]{2,1,0:T(4,128)(2,1)} %copy-done.15) | copy-start | bytes 786436
  156.9 1.9 copy-start.25
  157.0 1.9 copy-start.26
  157.2 1.7 copy-start.27
  158.9 1.5 copy-start.24
  160.3 5.0 %copy-start.23 = (bf16[128,4,128]{2,1,0:T(4,128)(2,1)S(1)}, bf16[128,4,128]{2,1,0:T(4,128)(2,1)}, u32[]{:S(2)}) copy-start(bf16[128,4,128]{2,1,0:T(4,128)(2,1)} %slice.313) | copy-start | bytes 393220
  162.7 5.4 %copy-start.1 = (f32[512,1,512]{2,1,0:T(1,128)S(1)}, f32[512,1,512]{2,1,0:T(1,128)}, u32[]{:S(2)}) copy-start(f32[512,1,512]{2,1,0:T(1,128)} %get-tuple-element.103) | copy-start | bytes 3145732
  170.1 36.5 %all-to-all-start.4 = ((bf16[8,64,1,512]{3,1,2,0:T(8,128)(2,1)}), bf16[8,64,1,512]{3,1,2,0:T(8,128)(2,1)}, u32[]{:S(2)}, u32[]{:S(2)}) async-start(bf16[8,64,1,512]{3,1,2,0:T(8,128)(2,1)} %bitcast.239), calls=%async_computation.4 | async-start | bytes 1048576 | tf_op jit(solution)/shard_map/all_to_all | solution.py:142
  174.9 72.1 %reduce-scatter.2.cloned.1.call-start = ((), (), s32[]{:S(2)}) async-start(), calls=%async_computation.9 | async-start | bytes 1310720 | tf_op jit(solution)/shard_map/reduce_scatter | solution.py:127
  184.4 3.3 %copy-start.22 = (bf16[128,4,128]{2,1,0:T(4,128)(2,1)S(1)}, bf16[128,4,128]{2,1,0:T(4,128)(2,1)}, u32[]{:S(2)}) copy-start(bf16[128,4,128]{2,1,0:T(4,128)(2,1)} %slice.321) | copy-start | bytes 393220
  185.6 4.9 %copy-start.20 = (bf16[128,4,128]{2,1,0:T(4,128)(2,1)S(1)}, bf16[128,4,128]{2,1,0:T(4,128)(2,1)}, u32[]{:S(2)}) copy-start(bf16[128,4,128]{2,1,0:T(4,128)(2,1)} %slice.329) | copy-start | bytes 393220
  185.6 17.1 %collective-permute-start.4 = (bf16[2048,256]{1,0:T(8,128)(2,1)}, bf16[2048,256]{1,0:T(8,128)(2,1)}, u32[]{:S(2)}, u32[]{:S(2)}) collective-permute-start(bf16[2048,256]{1,0:T(8,128)(2,1)} %fusion.61), channel_id=1, source_target_pairs={{0,1},{1,0},{2,3},{3,2},{4,5},{5,4},{6,7},{7,6},{8,9},{9,8},{10,11... | collective-permute-start | bytes 3145736 | tf_op jit(solution)/shard_map/ppermute | solution.py:10
  198.7 3.9 %copy-start = (f32[2048,1,256]{2,0,1:T(8,128)S(1)}, f32[2048,1,256]{2,0,1:T(8,128)}, u32[]{:S(2)}) copy-start(f32[2048,1,256]{2,0,1:T(8,128)} %copy.181) | copy-start | bytes 6291460
  202.7 2.8 %copy-start.2 = (f32[512,1,512]{2,1,0:T(1,128)S(1)}, f32[512,1,512]{2,1,0:T(1,128)}, u32[]{:S(2)}) copy-start(f32[512,1,512]{2,1,0:T(1,128)} %get-tuple-element.105) | copy-start | bytes 3145732
  202.7 2.8 %collective-permute-start.2 = (bf16[512,512]{1,0:T(8,128)(2,1)}, bf16[512,512]{1,0:T(8,128)(2,1)}, u32[]{:S(2)}, u32[]{:S(2)}) collective-permute-start(bf16[512,512]{1,0:T(8,128)(2,1)} %bitcast.234), channel_id=1, source_target_pairs={{0,1},{1,0},{2,3},{3,2},{4,5},{5,4},{6,7},{7,6},{8,9},{9,8},{10,11... | collective-permute-start | bytes 1572872 | tf_op jit(solution)/shard_map/ppermute | solution.py:10
  226.6 18.8 %all-to-all-start.6 = ((bf16[8,64,1,512]{3,1,2,0:T(8,128)(2,1)}), bf16[8,64,1,512]{3,1,2,0:T(8,128)(2,1)S(1)}, u32[]{:S(2)}, u32[]{:S(2)}) async-start(bf16[8,64,1,512]{3,1,2,0:T(8,128)(2,1)} %bitcast.60), calls=%async_computation.6 | async-start | bytes 1048576 | tf_op jit(solution)/shard_map/all_to_all | solution.py:144
Sparse Core Ops, SparseCore 0:
  205.5 28.9 reduce-scatter.1
where the time goes:
time: 258 us; the launch traced here: 256 us
  waiting for transfers between devices  62.4 us (24%)
  local copies, waits for them, and re-layouts  61.6 us (24%)
  matrix products  44 us (17%)
  starting transfers between devices  32.3 us (13%)
  other arithmetic  21 us (8%)
  blocking collectives  19.9 us (8%)
  between operations  14.5 us (6%)
    all_to_all x1, blocking collectives, body(): lax.all_to_all(to_tokens(key_grad), 'seq', split_axis=0, concat_axis=2, t...  19.9 us
    all_to_all x1, waiting for transfers between devices, body(): lax.all_to_all(to_heads(values), 'seq', split_axis=1, concat_axis=0, tile...  14 us
    all_to_all x1, waiting for transfers between devices, body(): lax.all_to_all(to_heads(out_grad), 'seq', split_axis=1, concat_axis=0, ti...  13.9 us
    all_to_all x1, waiting for transfers between devices, body(): lax.all_to_all(to_heads(key_vectors), 'seq', split_axis=1, concat_axis=0,...  13.2 us
    dot_general x4, matrix products, body(): jnp.einsum('hqk,qhd->khd', dscore, query_block, preferred_element_type=jn...  10.8 us
    all_to_all x1, waiting for transfers between devices, body(): lax.all_to_all(to_tokens(value_grad), 'seq', split_axis=0, concat_axis=2,...  10.8 us
    all_to_all x1, waiting for transfers between devices, body(): lax.all_to_all(to_heads(queries), 'seq', split_axis=1, concat_axis=0, til...  10.3 us
    dot_general x4, matrix products, body(): jnp.einsum('hqk,qhd->khd', probs_low, grad_block, preferred_element_type=...  9.58 us
  transfers between devices with their start and end apart: 13, of which 5 were waited for; matrix products, arithmetic and copies ran while one was open for 48% of the time, Pallas kernels for 0%

commit v1 on v0

--- a/solution.py
+++ b/solution.py
@@ -6,11 +6,40 @@
 HD = 128
 
 
+def register_corner(tile_in, join_dim, obj):
+    heard, local_part = (tile_in.shape[:join_dim], tile_in.shape[join_dim + 1 :])
+    clean = tile_in.reshape(*heard, obj, -1, *local_part)
+    return jnp.moveaxis(clean, join_dim, 0)
+
+
+def work_signs(z, pos_dim):
+    g_now = list(z.shape[1:])
+    g_now[pos_dim] *= z.shape[0]
+    return jnp.moveaxis(z, 0, pos_dim).reshape(g_now)
+
+
 def partner(value, axis, apart):
     return lax.ppermute(value, axis, [(i, i ^ 1 << apart) for i in range(lax.axis_size(axis))])
 
 
 def body(queries, key_vectors, values, out_grad, inputs):
+
+    def turn_the_lane(local_values, mesh_ax, field, block_here):
+        newest = lax.axis_size(mesh_ax)
+        local_now = lax.axis_index(mesh_ax)
+        reached, v1 = (newest, local_now)
+        state_now = register_corner(local_values, field, reached)
+        mid_arr = state_now
+        for j in range(1, reached):
+            raw_out, known = ((v1 + j) % reached, (v1 - j) % reached)
+            b_now = lax.dynamic_index_in_dim(state_now, raw_out, 0)
+            made = []
+            for m in range(reached):
+                made.append((m, (m + j) % reached))
+            aux = lax.ppermute(b_now, axis_name=mesh_ax, perm=made)
+            mid_arr = lax.dynamic_update_slice_in_dim(mid_arr, aux, known, axis=0)
+        return work_signs(mid_arr, block_here)
+
     seq_count = lax.axis_size("seq")
     groups = seq_count // 2
     parity = lax.axis_index("seq") % 2
@@ -40,7 +69,7 @@
         lax.all_to_all(to_heads(queries), "seq", split_axis=1, concat_axis=0, tiled=True),
         lax.all_to_all(to_heads(key_vectors), "seq", split_axis=1, concat_axis=0, tiled=True),
         lax.all_to_all(to_heads(values), "seq", split_axis=1, concat_axis=0, tiled=True),
-        lax.all_to_all(to_heads(out_grad), "seq", split_axis=1, concat_axis=0, tiled=True),
+        turn_the_lane(to_heads(out_grad), "seq", 1, 0),
     )
     q_rows = moved[0].reshape(own_rows, group_width)
     k_rows = moved[1].reshape(own_rows, group_width)

time: 258 us -> 239 us (0.926)
  waiting for transfers between devices: 62.4 us -> 41.7 us
  starting transfers between devices: 32.3 us -> 40.2 us
  local copies, waits for them, and re-layouts: 61.6 us -> 56.7 us
    all_to_all x1 -> x0, waiting for transfers between devices: 13.9 us -> none  [body(): lax.all_to_all(to_heads(out_grad), 'seq', split_axis=1, concat_axis=0, ti...]
    ppermute x0 -> x7, starting transfers between devices: none -> 10.8 us  [turn_the_lane(): aux = lax.ppermute(b_now, axis_name=mesh_ax, perm=made)]
    all_to_all x1, waiting for transfers between devices: 13.2 us -> 7.88 us  [body(): lax.all_to_all(to_heads(key_vectors), 'seq', split_axis=1, concat_axis=0,...]
    all_to_all x1 -> x0, starting transfers between devices: 3.63 us -> none  [body(): lax.all_to_all(to_heads(out_grad), 'seq', split_axis=1, concat_axis=0, ti...]
    all_to_all x1, waiting for transfers between devices: 14 us -> 11.1 us  [body(): lax.all_to_all(to_heads(values), 'seq', split_axis=1, concat_axis=0, tile...]
  transfers between devices with their start and end apart: 13 -> 19, of which waited for: 5 -> 4; matrix products, arithmetic and copies ran while one was open for 48% -> 49% of each run, Pallas kernels for 0% -> 0%
where the time goes in v1:
time: 239 us; the launch traced here: 238 us
  local copies, waits for them, and re-layouts  56.7 us (24%)
  matrix products  43.3 us (18%)
  waiting for transfers between devices  41.7 us (17%)
  starting transfers between devices  40.2 us (17%)
  other arithmetic  21 us (9%)
  blocking collectives  19.9 us (8%)
  between operations  14.7 us (6%)
    all_to_all x1, blocking collectives, body(): lax.all_to_all(to_tokens(key_grad), 'seq', split_axis=0, concat_axis=2, t...  19.9 us
    all_to_all x1, waiting for transfers between devices, body(): lax.all_to_all(to_heads(queries), 'seq', split_axis=1, concat_axis=0, til...  11.9 us
    all_to_all x1, waiting for transfers between devices, body(): lax.all_to_all(to_heads(values), 'seq', split_axis=1, concat_axis=0, tile...  11.1 us
    all_to_all x1, waiting for transfers between devices, body(): lax.all_to_all(to_tokens(value_grad), 'seq', split_axis=0, concat_axis=2,...  10.8 us
    ppermute x7, starting transfers between devices, turn_the_lane(): aux = lax.ppermute(b_now, axis_name=mesh_ax, perm=made)  10.8 us
    dot_general x4, matrix products, body(): jnp.einsum('hqk,qhd->khd', dscore, query_block, preferred_element_type=jn...  10.7 us
    dot_general x4, matrix products, body(): jnp.einsum('hqk,qhd->khd', probs_low, grad_block, preferred_element_type=...  9.76 us
    dot_general x4, matrix products, body(): jnp.einsum('hqk,khd->qhd', dscore, key_block, preferred_element_type=jnp....  8.84 us
  transfers between devices with their start and end apart: 19, of which 4 were waited for; matrix products, arithmetic and copies ran while one was open for 49% of the time, Pallas kernels for 0%

profile of v1, /device:TPU:0, one launch (start us, length us, event | category | flops | bytes accessed | tf_op | source)
XLA Modules:
  0.0 237.6 jit_solution(8235667664040158257)
XLA Ops:
  9.6 6.5 %all-to-all-start.2 = ((bf16[64,8,512]{2,0,1:T(8,128)(2,1)}), bf16[64,8,512]{2,0,1:T(8,128)(2,1)S(1)}, u32[]{:S(2)}, u32[]{:S(2)}) async-start(bf16[64,8,512]{2,0,1:T(8,128)(2,1)} %bitcast.25), calls=%async_computation.2 | async-start | bytes 1048576 | tf_op jit(solution)/shard_map/all_to_all | solution.py:71
  17.9 1.7 collective-permute-start.2
  19.6 2.2 collective-permute-start.3
  26.4 11.1 %all-to-all-done.2 = bf16[64,8,512]{2,0,1:T(8,128)(2,1)S(1)} async-done(((bf16[64,8,512]{2,0,1:T(8,128)(2,1)}), bf16[64,8,512]{2,0,1:T(8,128)(2,1)S(1)}, u32[]{:S(2)}, u32[]{:S(2)}) %all-to-all-start.2) | async-done | bytes 524320 | tf_op jit(solution)/shard_map/all_to_all | solution.py:71
  37.5 3.5 %all-to-all-start = ((bf16[64,8,512]{2,0,1:T(8,128)(2,1)}), bf16[64,8,512]{2,0,1:T(8,128)(2,1)S(1)}, u32[]{:S(2)}, u32[]{:S(2)}) async-start(bf16[64,8,512]{2,0,1:T(8,128)(2,1)} %bitcast.1), calls=%async_computation | async-start | bytes 1048576 | tf_op jit(solution)/shard_map/all_to_all | solution.py:70
  45.0 3.8 %collective-permute-start.6 = (bf16[1,64,1,512]{3,1,0,2:T(8,128)(2,1)}, bf16[1,64,1,512]{3,1,0,2:T(8,128)(2,1)S(1)}, u32[]{:S(2)}, u32[]{:S(2)}) collective-permute-start(bf16[1,64,1,512]{3,1,0,2:T(8,128)(2,1)} %get-tuple-element.127), channel_id=1, source_target_pairs={{0,6},{1,7},{2,0},{3,1},{4,2},{5,3},{6,4},{7,5},{8,14},{9,15},{10,... | collective-permute-start | bytes 196616 | tf_op jit(solution)/shard_map/ppermute | solution.py:39
  48.9 7.9 %all-to-all-done = bf16[64,8,512]{2,0,1:T(8,128)(2,1)S(1)} async-done(((bf16[64,8,512]{2,0,1:T(8,128)(2,1)}), bf16[64,8,512]{2,0,1:T(8,128)(2,1)S(1)}, u32[]{:S(2)}, u32[]{:S(2)}) %all-to-all-start) | async-done | bytes 524320 | tf_op jit(solution)/shard_map/all_to_all | solution.py:70
  56.8 4.2 %all-to-all-start.1 = ((bf16[64,8,512]{2,0,1:T(8,128)(2,1)}), bf16[64,8,512]{2,0,1:T(8,128)(2,1)S(1)}, u32[]{:S(2)}, u32[]{:S(2)}) async-start(bf16[64,8,512]{2,0,1:T(8,128)(2,1)} %bitcast.10), calls=%async_computation.1 | async-start | bytes 1048576 | tf_op jit(solution)/shard_map/all_to_all | solution.py:69
  64.4 11.9 %all-to-all-done.1 = bf16[64,8,512]{2,0,1:T(8,128)(2,1)S(1)} async-done(((bf16[64,8,512]{2,0,1:T(8,128)(2,1)}), bf16[64,8,512]{2,0,1:T(8,128)(2,1)S(1)}, u32[]{:S(2)}, u32[]{:S(2)}) %all-to-all-start.1) | async-done | bytes 524320 | tf_op jit(solution)/shard_map/all_to_all | solution.py:69
  76.3 1.6 broadcast_in_dim.67
  77.9 3.8 %all-to-all-start.6 = ((bf16[64,8,2048]{2,0,1:T(8,128)(2,1)}), bf16[64,8,2048]{2,0,1:T(8,128)(2,1)S(1)}, u32[]{:S(2)}, u32[]{:S(2)}) async-start(bf16[64,8,2048]{2,0,1:T(8,128)(2,1)} %bitcast.66), calls=%async_computation.6 | async-start | bytes 4194304 | tf_op jit(solution)/shard_map/all_to_all | solution.py:147
  81.7 1.8 fusion.215
  83.5 1.6 slice.329
  93.7 2.1 fusion.232
  95.8 2.3 convolution_bitcast_fusion.3
  98.1 2.6 %scatter-add.34 = f32[1024,4,128]{0,2,1:T(8,128)} pad(f32[256,4,128]{0,2,1:T(8,128)} %convolution_bitcast_fusion.3, f32[]{:T(128)} %constant.305.clone.1), padding=0_768x0_0x0_0 | pad | bytes 2621444 | tf_op jit(solution)/shard_map/scatter-add | solution.py:126
  100.7 2.1 fusion.217
  102.8 2.2 fusion.227
  105.0 2.4 %fusion.17 = f32[1024,4,128]{0,2,1:T(8,128)} fusion(f32[1024,4,128]{0,2,1:T(8,128)} %scatter-add.34, bf16[128,4,128]{0,2,1:T(8,128)(2,1)S(1)} %copy-done.8, f32[4,128]{1,0:T(4,128)S(1)} %get-tuple-element.137, pred[128,256]{0,1:T(8,128)(4,1)} %broadcast_compare_fusion.2, bf16[256,4,128]{2,1,0:T(4,128)(2,1)} %slice.311, bf16[128,4,128]{2,1,0:T(4,128)(2,1)} %slice.313), kind=kOutput, calls=%fused_computation.38 | convolution fusion | flops 67764992 | bytes 1083392 | tf_op jit(solution)/shard_map/hqk,qhd->khd/dot_general | solution.py:127
  107.9 1.9 fusion.222
  109.8 2.4 %fusion.24 = f32[1024,4,128]{0,2,1:T(8,128)} fusion(f32[1024,4,128]{0,2,1:T(8,128)} %fusion.17, bf16[128,4,128]{0,2,1:T(8,128)(2,1)S(1)} %copy-done.10, f32[4,128]{1,0:T(4,128)S(1)} %get-tuple-element.135, pred[128,256]{0,1:T(8,128)(4,1)} %broadcast_compare_fusion.1, bf16[256,4,128]{2,1,0:T(4,128)(2,1)S(1)} %slice.319, bf16[128,4,128]{2,1,0:T(4,128)(2,1)S(1)} %copy-done.22), kind=kOutput, calls=%fused_computation.50 | convolution fusion | flops 67896064 | bytes 1607680 | tf_op jit(solution)/shard_map/hqk,qhd->khd/dot_general | solution.py:127
  117.4 2.6 %fusion.26 = f32[1024,4,128]{0,2,1:T(8,128)} fusion(f32[1024,4,128]{0,2,1:T(8,128)} %fusion.24, bf16[128,4,128]{0,2,1:T(8,128)(2,1)} %copy.221, f32[4,128]{1,0:T(4,128)S(1)} %get-tuple-element.133, pred[128,256]{0,1:T(8,128)(4,1)} %broadcast_compare_fusion, bf16[256,4,128]{2,1,0:T(4,128)(2,1)} %slice.327, bf16[128,4,128]{2,1,0:T(4,128)(2,1)} %slice.329), kind=kOutput, calls=%fused_computation.52 | convolution fusion | flops 67896064 | bytes 1607680 | tf_op jit(solution)/shard_map/hqk,qhd->khd/dot_general | solution.py:127
  120.0 2.8 %copy.223 = bf16[1024,4,128]{2,1,0:T(4,128)(2,1)} copy(f32[1024,4,128]{0,2,1:T(8,128)} %fusion.26) | data formatting | bytes 3145728 | tf_op jit(solution)/shard_map/scatter-add | solution.py:126
  124.3 3.0 %fusion.60 = (bf16[512,1,512]{2,1,0:T(2,128)(2,1)S(1)}, f32[512,1,512]{2,1,0:T(1,128)}) fusion(pred[]{:T(512)S(6)} %eq.19, bf16[512,2,512]{2,1,0:T(2,128)(2,1)S(1)} %reshape.500), kind=kLoop, calls=%fused_computation.94 | loop fusion | flops 786432 | bytes 2621441 | tf_op jit(solution)/shard_map/convert_element_type | solution.py:135
  128.7 2.4 %fusion.54 = bf16[128,4,128]{2,0,1:T(8,128)(2,1)} fusion(f32[4,128,256]{1,2,0:T(8,128)S(1)} %fusion.86, bf16[256,4,128]{2,1,0:T(4,128)(2,1)S(1)} %copy-done.18, f32[4,128,256]{1,2,0:T(8,128)} %get-tuple-element.134, f32[4,128]{1,0:T(4,128)S(1)} %get-tuple-element.133), kind=kOutput, calls=%fused_computation.88 | convolution fusion | flops 34538240 | bytes 1443840 | tf_op jit(solution)/shard_map/hqk,khd->qhd/dot_general | solution.py:119
  131.2 2.0 fusion.88
  133.1 2.0 fusion.53
  136.2 2.8 %fusion.52 = bf16[128,4,128]{2,0,1:T(8,128)(2,1)} fusion(f32[4,128,256]{1,2,0:T(8,128)} %fusion.90, bf16[256,4,128]{2,1,0:T(4,128)(2,1)} %slice.311, f32[4,128,256]{1,2,0:T(8,128)} %get-tuple-element.138, f32[4,128]{1,0:T(4,128)S(1)} %get-tuple-element.137), kind=kOutput, calls=%fused_computation.86 | convolution fusion | flops 34538240 | bytes 1443840 | tf_op jit(solution)/shard_map/hqk,khd->qhd/dot_general | solution.py:119
  139.2 1.6 fusion.51
  142.3 2.4 convolution_bitcast_fusion.7
  144.7 2.6 %scatter-add.26 = f32[1024,4,128]{2,0,1:T(8,128)} pad(f32[256,4,128]{2,0,1:T(8,128)} %convolution_bitcast_fusion.7, f32[]{:T(128)} %constant.305.clone.1), padding=0_768x0_0x0_0 | pad | bytes 2621444 | tf_op jit(solution)/shard_map/scatter-add | solution.py:123
  147.2 2.8 %fusion.18 = f32[1024,4,128]{2,0,1:T(8,128)} fusion(f32[1024,4,128]{2,0,1:T(8,128)} %scatter-add.26, f32[4,128,256]{1,2,0:T(8,128)} %fusion.90, bf16[128,4,128]{2,1,0:T(4,128)(2,1)S(1)} %copy-done.24, f32[4,128,256]{1,2,0:T(8,128)} %get-tuple-element.138, f32[4,128]{1,0:T(4,128)S(1)} %get-tuple-element.137), kind=kOutput, calls=%fused_computation.43 | convolution fusion | flops 34472704 | bytes 2756608 | tf_op jit(solution)/shard_map/hqk,qhd->khd/dot_general | solution.py:124
  150.0 2.1 fusion.62
  152.1 4.8 %all-to-all-start.3 = ((bf16[8,64,1,512]{3,1,2,0:T(8,128)(2,1)}), bf16[8,64,1,512]{3,1,2,0:T(8,128)(2,1)}, u32[]{:S(2)}, u32[]{:S(2)}) async-start(bf16[8,64,1,512]{3,1,2,0:T(8,128)(2,1)} %bitcast.254), calls=%async_computation.3 | async-start | bytes 1048576 | tf_op jit(solution)/shard_map/all_to_all | solution.py:171
  156.9 2.3 fusion.237
  159.3 2.2 fusion.214
  161.5 1.9 copy.246
  163.4 2.9 %copy.245 = f32[2048,1,256]{2,0,1:T(8,128)} copy(f32[2048,1,256]{0,2,1:T(8,128)} %get-tuple-element.100) | data formatting | bytes 4194304
  167.6 2.1 collective-permute-start.11
  169.7 2.8 %fusion.20 = f32[1024,4,128]{2,0,1:T(8,128)} fusion(f32[1024,4,128]{2,0,1:T(8,128)} %fusion.18, f32[4,128,256]{1,2,0:T(8,128)} %fusion.88, bf16[128,4,128]{2,1,0:T(4,128)(2,1)S(1)} %copy-done.23, f32[4,128,256]{1,2,0:T(8,128)} %get-tuple-element.136, f32[4,128]{1,0:T(4,128)S(1)} %get-tuple-element.135), kind=kOutput, calls=%fused_computation.46 | convolution fusion | flops 34603776 | bytes 3280896 | tf_op jit(solution)/shard_map/hqk,qhd->khd/dot_general | solution.py:124
  172.5 2.8 %fusion.22 = f32[1024,4,128]{2,0,1:T(8,128)} fusion(f32[1024,4,128]{2,0,1:T(8,128)} %fusion.20, f32[4,128,256]{1,2,0:T(8,128)} %copy-done.7, bf16[128,4,128]{2,1,0:T(4,128)(2,1)S(1)} %copy-done.21, f32[4,128,256]{1,2,0:T(8,128)} %get-tuple-element.134, f32[4,128]{1,0:T(4,128)S(1)} %get-tuple-element.133), kind=kOutput, calls=%fused_computation.48 | convolution fusion | flops 34603776 | bytes 3280896 | tf_op jit(solution)/shard_map/hqk,qhd->khd/dot_general | solution.py:124
  175.3 3.9 %copy.212 = bf16[1024,4,128]{2,1,0:T(4,128)(2,1)} copy(f32[1024,4,128]{2,0,1:T(8,128)} %fusion.22) | data formatting | bytes 3145728 | tf_op jit(solution)/shard_map/scatter-add | solution.py:123
  180.7 3.0 %fusion.57 = (bf16[512,1,512]{2,1,0:T(2,128)(2,1)S(1)}, f32[512,1,512]{2,1,0:T(1,128)}) fusion(pred[]{:T(512)S(6)} %eq.19, bf16[512,2,512]{2,1,0:T(2,128)(2,1)S(1)} %reshape.496), kind=kLoop, calls=%fused_computation.91 | loop fusion | flops 786432 | bytes 2621441 | tf_op jit(solution)/shard_map/convert_element_type | solution.py:135
  184.7 2.7 %fusion.8 = bf16[2048,256]{1,0:T(8,128)(2,1)} fusion(bf16[2048,256]{1,0:T(8,128)(2,1)} %collective-permute-done.11, f32[2048,1,256]{2,0,1:T(8,128)S(1)} %copy-done, f32[2048,1,256]{2,0,1:T(8,128)S(1)} %copy.246, pred[]{:T(512)S(6)} %eq.19), kind=kLoop, calls=%fused_computation.9 | loop fusion | flops 2097152 | bytes 6291457 | tf_op jit(solution)/shard_map/convert_element_type | solution.py:157
  188.7 19.9 %all_to_all.105 = bf16[8,64,1,512]{3,1,2,0:T(8,128)(2,1)S(1)} all-to-all(bf16[8,64,1,512]{3,1,2,0:T(8,128)(2,1)S(1)} %bitcast.262), channel_id=1, replica_groups=mesh['dp'=4,'seq'=8] {'seq'}, dimensions={0} | all-to-all | bytes 1048576 | tf_op jit(solution)/shard_map/all_to_all | solution.py:172
  208.6 3.8 %all-to-all-start.5 = ((bf16[8,64,1,512]{3,1,2,0:T(8,128)(2,1)}), bf16[8,64,1,512]{3,1,2,0:T(8,128)(2,1)S(1)}, u32[]{:S(2)}, u32[]{:S(2)}) async-start(bf16[8,64,1,512]{3,1,2,0:T(8,128)(2,1)} %bitcast.61), calls=%async_computation.5 | async-start | bytes 1048576 | tf_op jit(solution)/shard_map/all_to_all | solution.py:173
  216.6 10.8 %all-to-all-done.5 = bf16[8,64,1,512]{3,1,2,0:T(8,128)(2,1)S(1)} async-done(((bf16[8,64,1,512]{3,1,2,0:T(8,128)(2,1)}), bf16[8,64,1,512]{3,1,2,0:T(8,128)(2,1)S(1)}, u32[]{:S(2)}, u32[]{:S(2)}) %all-to-all-start.5) | async-done | bytes 524320 | tf_op jit(solution)/shard_map/all_to_all | solution.py:173
  229.0 1.8 convert_element_type.141
  (158 shorter events, 46.6 us)
Async XLA Ops:
  7.2 8.9 %copy-start.12 = (bf16[1,128,2048]{2,1,0:T(8,128)(2,1)S(1)}, bf16[1,128,2048]{2,1,0:T(8,128)(2,1)}, u32[]{:S(2)}) copy-start(bf16[1,128,2048]{2,1,0:T(8,128)(2,1)} %param.24) | copy-start | bytes 1572868
  9.6 14.7 %copy-start.13 = (bf16[1,128,2048]{2,1,0:T(8,128)(2,1)S(1)}, bf16[1,128,2048]{2,1,0:T(8,128)(2,1)}, u32[]{:S(2)}) copy-start(bf16[1,128,2048]{2,1,0:T(8,128)(2,1)} %param.22) | copy-start | bytes 1572868
  9.6 27.9 %all-to-all-start.2 = ((bf16[64,8,512]{2,0,1:T(8,128)(2,1)}), bf16[64,8,512]{2,0,1:T(8,128)(2,1)S(1)}, u32[]{:S(2)}, u32[]{:S(2)}) async-start(bf16[64,8,512]{2,0,1:T(8,128)(2,1)} %bitcast.25), calls=%async_computation.2 | async-start | bytes 1048576 | tf_op jit(solution)/shard_map/all_to_all | solution.py:71
  16.7 26.5 %copy-start.14 = (bf16[1,128,2048]{2,1,0:T(8,128)(2,1)S(1)}, bf16[1,128,2048]{2,1,0:T(8,128)(2,1)}, u32[]{:S(2)}) copy-start(bf16[1,128,2048]{2,1,0:T(8,128)(2,1)} %param.21) | copy-start | bytes 1572868
  17.4 27.6 %collective-permute-start.1 = (bf16[1,64,1,512]{3,1,0,2:T(8,128)(2,1)}, bf16[1,64,1,512]{3,1,0,2:T(8,128)(2,1)S(1)}, u32[]{:S(2)}, u32[]{:S(2)}) collective-permute-start(bf16[1,64,1,512]{3,1,0,2:T(8,128)(2,1)} %get-tuple-element.132), channel_id=1, source_target_pairs={{0,1},{1,2},{2,3},{3,4},{4,5},{5,6},{6,7},{7,0},{8,9},{9,10},{10,1... | collective-permute-start | bytes 196616 | tf_op jit(solution)/shard_map/ppermute | solution.py:39
  17.9 30.9 %collective-permute-start.2 = (bf16[1,64,1,512]{3,1,0,2:T(8,128)(2,1)}, bf16[1,64,1,512]{3,1,0,2:T(8,128)(2,1)S(1)}, u32[]{:S(2)}, u32[]{:S(2)}) collective-permute-start(bf16[1,64,1,512]{3,1,0,2:T(8,128)(2,1)} %get-tuple-element.131), channel_id=1, source_target_pairs={{0,2},{1,3},{2,4},{3,5},{4,6},{5,7},{6,0},{7,1},{8,10},{9,11},{10,... | collective-permute-start | bytes 196616 | tf_op jit(solution)/shard_map/ppermute | solution.py:39
  19.6 41.4 %collective-permute-start.3 = (bf16[1,64,1,512]{3,1,0,2:T(8,128)(2,1)}, bf16[1,64,1,512]{3,1,0,2:T(8,128)(2,1)S(1)}, u32[]{:S(2)}, u32[]{:S(2)}) collective-permute-start(bf16[1,64,1,512]{3,1,0,2:T(8,128)(2,1)} %get-tuple-element.130), channel_id=1, source_target_pairs={{0,3},{1,4},{2,5},{3,6},{4,7},{5,0},{6,1},{7,2},{8,11},{9,12},{10,... | collective-permute-start | bytes 196616 | tf_op jit(solution)/shard_map/ppermute | solution.py:39
  21.8 39.2 %collective-permute-start.4 = (bf16[1,64,1,512]{3,1,0,2:T(8,128)(2,1)}, bf16[1,64,1,512]{3,1,0,2:T(8,128)(2,1)S(1)}, u32[]{:S(2)}, u32[]{:S(2)}) collective-permute-start(bf16[1,64,1,512]{3,1,0,2:T(8,128)(2,1)} %get-tuple-element.129), channel_id=1, source_target_pairs={{0,4},{1,5},{2,6},{3,7},{4,0},{5,1},{6,2},{7,3},{8,12},{9,13},{10,... | collective-permute-start | bytes 196616 | tf_op jit(solution)/shard_map/ppermute | solution.py:39
  23.3 37.7 %collective-permute-start.5 = (bf16[1,64,1,512]{3,1,0,2:T(8,128)(2,1)}, bf16[1,64,1,512]{3,1,0,2:T(8,128)(2,1)S(1)}, u32[]{:S(2)}, u32[]{:S(2)}) collective-permute-start(bf16[1,64,1,512]{3,1,0,2:T(8,128)(2,1)} %get-tuple-element.128), channel_id=1, source_target_pairs={{0,5},{1,6},{2,7},{3,0},{4,1},{5,2},{6,3},{7,4},{8,13},{9,14},{10,... | collective-permute-start | bytes 196616 | tf_op jit(solution)/shard_map/ppermute | solution.py:39
  24.7 19.8 %copy-start.15 = (bf16[1,128,2048]{2,1,0:T(8,128)(2,1)S(1)}, bf16[1,128,2048]{2,1,0:T(8,128)(2,1)}, u32[]{:S(2)}) copy-start(bf16[1,128,2048]{2,1,0:T(8,128)(2,1)} %param.25) | copy-start | bytes 1572868
  37.5 19.3 %all-to-all-start = ((bf16[64,8,512]{2,0,1:T(8,128)(2,1)}), bf16[64,8,512]{2,0,1:T(8,128)(2,1)S(1)}, u32[]{:S(2)}, u32[]{:S(2)}) async-start(bf16[64,8,512]{2,0,1:T(8,128)(2,1)} %bitcast.1), calls=%async_computation | async-start | bytes 1048576 | tf_op jit(solution)/shard_map/all_to_all | solution.py:70
  45.0 16.0 %collective-permute-start.6 = (bf16[1,64,1,512]{3,1,0,2:T(8,128)(2,1)}, bf16[1,64,1,512]{3,1,0,2:T(8,128)(2,1)S(1)}, u32[]{:S(2)}, u32[]{:S(2)}) collective-permute-start(bf16[1,64,1,512]{3,1,0,2:T(8,128)(2,1)} %get-tuple-element.127), channel_id=1, source_target_pairs={{0,6},{1,7},{2,0},{3,1},{4,2},{5,3},{6,4},{7,5},{8,14},{9,15},{10,... | collective-permute-start | bytes 196616 | tf_op jit(solution)/shard_map/ppermute | solution.py:39
  48.8 12.8 %collective-permute-start.7 = (bf16[1,64,1,512]{3,1,0,2:T(8,128)(2,1)S(1)}, bf16[1,64,1,512]{3,1,0,2:T(8,128)(2,1)S(1)}, u32[]{:S(2)}, u32[]{:S(2)}) collective-permute-start(bf16[1,64,1,512]{3,1,0,2:T(8,128)(2,1)S(1)} %get-tuple-element.126), channel_id=1, source_target_pairs={{0,7},{1,0},{2,1},{3,2},{4,3},{5,4},{6,5},{7,6},{8,15},{9,8},{10,9... | collective-permute-start | bytes 196616 | tf_op jit(solution)/shard_map/ppermute | solution.py:39
  56.8 19.5 %all-to-all-start.1 = ((bf16[64,8,512]{2,0,1:T(8,128)(2,1)}), bf16[64,8,512]{2,0,1:T(8,128)(2,1)S(1)}, u32[]{:S(2)}, u32[]{:S(2)}) async-start(bf16[64,8,512]{2,0,1:T(8,128)(2,1)} %bitcast.10), calls=%async_computation.1 | async-start | bytes 1048576 | tf_op jit(solution)/shard_map/all_to_all | solution.py:69
  61.1 27.1 %collective-permute-start = (bf16[512,512]{1,0:T(8,128)(2,1)S(1)}, bf16[512,512]{1,0:T(8,128)(2,1)}, u32[]{:S(2)}, u32[]{:S(2)}) collective-permute-start(bf16[512,512]{1,0:T(8,128)(2,1)S(1)} %bitcast.253), channel_id=1, source_target_pairs={{0,1},{1,0},{2,3},{3,2},{4,5},{5,4},{6,7},{7,6},{8,9},{9,8},{10,11... | collective-permute-start | bytes 1572872 | tf_op jit(solution)/shard_map/ppermute | solution.py:22
  64.3 47.9 %collective-permute-start.8 = (bf16[512,512]{1,0:T(8,128)(2,1)S(1)}, bf16[512,512]{1,0:T(8,128)(2,1)}, u32[]{:S(2)}, u32[]{:S(2)}) collective-permute-start(bf16[512,512]{1,0:T(8,128)(2,1)S(1)} %bitcast.252), channel_id=1, source_target_pairs={{0,1},{1,0},{2,3},{3,2},{4,5},{5,4},{6,7},{7,6},{8,9},{9,8},{10,11... | collective-permute-start | bytes 1572872 | tf_op jit(solution)/shard_map/ppermute | solution.py:22
  76.3 1.6 copy-start.3
  77.9 74.2 %all-to-all-start.6 = ((bf16[64,8,2048]{2,0,1:T(8,128)(2,1)}), bf16[64,8,2048]{2,0,1:T(8,128)(2,1)S(1)}, u32[]{:S(2)}, u32[]{:S(2)}) async-start(bf16[64,8,2048]{2,0,1:T(8,128)(2,1)} %bitcast.66), calls=%async_computation.6 | async-start | bytes 4194304 | tf_op jit(solution)/shard_map/all_to_all | solution.py:147
  93.7 7.0 %copy-start.16 = (bf16[256,4,128]{2,1,0:T(4,128)(2,1)}, bf16[256,4,128]{2,1,0:T(4,128)(2,1)S(1)}, u32[]{:S(2)}) copy-start(bf16[256,4,128]{2,1,0:T(4,128)(2,1)S(1)} %slice.303) | copy-start | bytes 786436
  95.8 4.9 %copy-start.20 = (bf16[128,4,128]{2,1,0:T(4,128)(2,1)S(1)}, bf16[128,4,128]{2,1,0:T(4,128)(2,1)}, u32[]{:S(2)}) copy-start(bf16[128,4,128]{2,1,0:T(4,128)(2,1)} %slice.329) | copy-start | bytes 393220
  100.7 4.3 %copy-start.8 = (bf16[128,4,128]{0,2,1:T(8,128)(2,1)S(1)}, bf16[128,4,128]{0,2,1:T(8,128)(2,1)}, u32[]{:S(2)}) copy-start(bf16[128,4,128]{0,2,1:T(8,128)(2,1)} %copy.217) | copy-start | bytes 393220
  105.0 2.9 %copy-start.22 = (bf16[128,4,128]{2,1,0:T(4,128)(2,1)S(1)}, bf16[128,4,128]{2,1,0:T(4,128)(2,1)}, u32[]{:S(2)}) copy-start(bf16[128,4,128]{2,1,0:T(4,128)(2,1)} %slice.321) | copy-start | bytes 393220
  105.0 4.8 %copy-start.10 = (bf16[128,4,128]{0,2,1:T(8,128)(2,1)S(1)}, bf16[128,4,128]{0,2,1:T(8,128)(2,1)}, u32[]{:S(2)}) copy-start(bf16[128,4,128]{0,2,1:T(8,128)(2,1)} %copy.219) | copy-start | bytes 393220
  107.9 4.3 %copy-start.19 = (bf16[256,4,128]{2,1,0:T(4,128)(2,1)}, bf16[256,4,128]{2,1,0:T(4,128)(2,1)S(1)}, u32[]{:S(2)}) copy-start(bf16[256,4,128]{2,1,0:T(4,128)(2,1)S(1)} %slice.319) | copy-start | bytes 786436
  124.3 4.2 %copy-start.6 = (bf16[256,4,128]{2,1,0:T(4,128)(2,1)S(1)}, bf16[256,4,128]{2,1,0:T(4,128)(2,1)}, u32[]{:S(2)}) copy-start(bf16[256,4,128]{2,1,0:T(4,128)(2,1)} %slice.333) | copy-start | bytes 786436
  124.3 4.2 %copy-start.11 = (bf16[128,4,128]{0,2,1:T(8,128)(2,1)S(1)}, bf16[128,4,128]{0,2,1:T(8,128)(2,1)}, u32[]{:S(2)}) copy-start(bf16[128,4,128]{0,2,1:T(8,128)(2,1)} %copy.221) | copy-start | bytes 393220
  127.3 1.4 copy-start.18
  128.3 2.9 %copy-start.5 = (bf16[256,4,128]{2,1,0:T(4,128)(2,1)S(1)}, bf16[256,4,128]{2,1,0:T(4,128)(2,1)}, u32[]{:S(2)}) copy-start(bf16[256,4,128]{2,1,0:T(4,128)(2,1)} %slice.325) | copy-start | bytes 786436
  128.3 21.7 %collective-permute-start.10 = (bf16[512,512]{1,0:T(8,128)(2,1)}, bf16[512,512]{1,0:T(8,128)(2,1)}, u32[]{:S(2)}, u32[]{:S(2)}) collective-permute-start(bf16[512,512]{1,0:T(8,128)(2,1)} %bitcast.246), channel_id=1, source_target_pairs={{0,1},{1,0},{2,3},{3,2},{4,5},{5,4},{6,7},{7,6},{8,9},{9,8},{10,11... | collective-permute-start | bytes 1572872 | tf_op jit(solution)/shard_map/ppermute | solution.py:22
  128.7 6.5 %copy-start.7 = (f32[4,128,256]{1,2,0:T(8,128)}, f32[4,128,256]{1,2,0:T(8,128)S(1)}, u32[]{:S(2)}) copy-start(f32[4,128,256]{1,2,0:T(8,128)S(1)} %fusion.86) | copy-start | bytes 1572868
  131.2 4.0 %copy-start.4 = (bf16[256,4,128]{2,1,0:T(4,128)(2,1)S(1)}, bf16[256,4,128]{2,1,0:T(4,128)(2,1)}, u32[]{:S(2)}) copy-start(bf16[256,4,128]{2,1,0:T(4,128)(2,1)} %slice.317) | copy-start | bytes 786436
  133.1 2.1 copy-start.9
  136.2 3.0 %copy-start.17 = (bf16[256,4,128]{2,1,0:T(4,128)(2,1)S(1)}, bf16[256,4,128]{2,1,0:T(4,128)(2,1)}, u32[]{:S(2)}) copy-start(bf16[256,4,128]{2,1,0:T(4,128)(2,1)} %copy-done.16) | copy-start | bytes 786436
  139.0 1.9 copy-start.26
  139.2 1.6 copy-start.27
  140.8 1.5 copy-start.25
  142.3 4.9 %copy-start.24 = (bf16[128,4,128]{2,1,0:T(4,128)(2,1)S(1)}, bf16[128,4,128]{2,1,0:T(4,128)(2,1)}, u32[]{:S(2)}) copy-start(bf16[128,4,128]{2,1,0:T(4,128)(2,1)} %slice.313) | copy-start | bytes 393220
  144.7 5.3 %copy-start.1 = (f32[512,1,512]{2,1,0:T(1,128)S(1)}, f32[512,1,512]{2,1,0:T(1,128)}, u32[]{:S(2)}) copy-start(f32[512,1,512]{2,1,0:T(1,128)} %get-tuple-element.103) | copy-start | bytes 3145732
  152.1 36.5 %all-to-all-start.3 = ((bf16[8,64,1,512]{3,1,2,0:T(8,128)(2,1)}), bf16[8,64,1,512]{3,1,2,0:T(8,128)(2,1)}, u32[]{:S(2)}, u32[]{:S(2)}) async-start(bf16[8,64,1,512]{3,1,2,0:T(8,128)(2,1)} %bitcast.254), calls=%async_computation.3 | async-start | bytes 1048576 | tf_op jit(solution)/shard_map/all_to_all | solution.py:171
  156.9 72.1 %reduce-scatter.2.cloned.1.call-start = ((), (), s32[]{:S(2)}) async-start(), calls=%async_computation.8 | async-start | bytes 1310720 | tf_op jit(solution)/shard_map/reduce_scatter | solution.py:156
  166.4 3.3 %copy-start.23 = (bf16[128,4,128]{2,1,0:T(4,128)(2,1)S(1)}, bf16[128,4,128]{2,1,0:T(4,128)(2,1)}, u32[]{:S(2)}) copy-start(bf16[128,4,128]{2,1,0:T(4,128)(2,1)} %slice.321) | copy-start | bytes 393220
  167.6 4.9 %copy-start.21 = (bf16[128,4,128]{2,1,0:T(4,128)(2,1)S(1)}, bf16[128,4,128]{2,1,0:T(4,128)(2,1)}, u32[]{:S(2)}) copy-start(bf16[128,4,128]{2,1,0:T(4,128)(2,1)} %slice.329) | copy-start | bytes 393220
  167.6 17.1 %collective-permute-start.11 = (bf16[2048,256]{1,0:T(8,128)(2,1)}, bf16[2048,256]{1,0:T(8,128)(2,1)}, u32[]{:S(2)}, u32[]{:S(2)}) collective-permute-start(bf16[2048,256]{1,0:T(8,128)(2,1)} %fusion.61), channel_id=1, source_target_pairs={{0,1},{1,0},{2,3},{3,2},{4,5},{5,4},{6,7},{7,6},{8,9},{9,8},{10,11... | collective-permute-start | bytes 3145736 | tf_op jit(solution)/shard_map/ppermute | solution.py:22
  180.7 3.9 %copy-start = (f32[2048,1,256]{2,0,1:T(8,128)S(1)}, f32[2048,1,256]{2,0,1:T(8,128)}, u32[]{:S(2)}) copy-start(f32[2048,1,256]{2,0,1:T(8,128)} %copy.245) | copy-start | bytes 6291460
  184.6 2.8 %copy-start.2 = (f32[512,1,512]{2,1,0:T(1,128)S(1)}, f32[512,1,512]{2,1,0:T(1,128)}, u32[]{:S(2)}) copy-start(f32[512,1,512]{2,1,0:T(1,128)} %get-tuple-element.105) | copy-start | bytes 3145732
  184.6 2.7 %collective-permute-start.9 = (bf16[512,512]{1,0:T(8,128)(2,1)}, bf16[512,512]{1,0:T(8,128)(2,1)}, u32[]{:S(2)}, u32[]{:S(2)}) collective-permute-start(bf16[512,512]{1,0:T(8,128)(2,1)} %bitcast.247), channel_id=1, source_target_pairs={{0,1},{1,0},{2,3},{3,2},{4,5},{5,4},{6,7},{7,6},{8,9},{9,8},{10,11... | collective-permute-start | bytes 1572872 | tf_op jit(solution)/shard_map/ppermute | solution.py:22
  208.6 18.8 %all-to-all-start.5 = ((bf16[8,64,1,512]{3,1,2,0:T(8,128)(2,1)}), bf16[8,64,1,512]{3,1,2,0:T(8,128)(2,1)S(1)}, u32[]{:S(2)}, u32[]{:S(2)}) async-start(bf16[8,64,1,512]{3,1,2,0:T(8,128)(2,1)} %bitcast.61), calls=%async_computation.5 | async-start | bytes 1048576 | tf_op jit(solution)/shard_map/all_to_all | solution.py:173
Sparse Core Ops, SparseCore 0:
  187.5 28.8 reduce-scatter.1
